TPU v7x, 256 devices: a whole 4x4x8 slice. The times are simulated.
256 devices in a mesh: fsdp: 64 (over x, y, z_hi), tp: 4 (over z_lo, core).
Axes of the slice: x: 4, y: 4, z: 8 (z_hi: 4, z_lo: 2; z = z_hi * 2 + z_lo), core: 2. Of those that a mesh axis runs over, the one named last changes fastest.
Arguments:
- momentum: float32 [14336, 4096], P('fsdp', 'tp'), may hold values from -6 to 6
- grad_acc: float32 [14336, 4096], P('fsdp', 'tp'), may hold values from -6 to 6
- query_basis: float32 [4096, 512], P('tp'), may hold values from -6 to 6
- hidden_t: bfloat16 [14336, 8192], P(None, 'fsdp'), may hold values from -6 to 6
- out_grad: bfloat16 [8192, 4096], P('fsdp', 'tp'), may hold values from -0.0625 to 0.0625
Outputs:
- update: float32 [14336, 4096], P('fsdp', 'tp')
- momentum_next: float32 [14336, 4096], P('fsdp', 'tp')
- query_next: float32 [4096, 512], P('tp')
All inputs are finite; a program needn't handle non-finite values.
Results may differ from a plain program's by a relative error of at most 0.0003.
Values may be sent and summed in bfloat16 or wider, within the bound.
No kernel may reach another device: no remote copies, remote signals or barrier semaphores. Data moves between devices by JAX's collectives and lax.ppermute only.
A program may use at most 128 MiB of HBM per device.

v0:
```python
import math

import jax
import jax.numpy as jnp
from jax import lax
from jax.sharding import PartitionSpec as P

D = 4096
FF = 14336
RANK = 512


momentum_keep = 0.95
epsilon = 1e-06


def from_everyone(shard, axis):
    devices = lax.axis_size(axis)
    return lax.all_to_all(
        jnp.broadcast_to(shard[None], (devices, *shard.shape)), axis, 0, 0, tiled=True
    )


def over_copies(shard, axis):
    return from_everyone(shard, axis).sum(axis=0)


def rows_for(lines, devices):
    spare = -len(lines) % devices
    return jnp.pad(lines, [(0, spare)] + [(0, 0)] * (lines.ndim - 1))


def in_order(pieces, dim):
    shape = list(pieces.shape[1:])
    shape[dim] *= pieces.shape[0]
    return jnp.moveaxis(pieces, 0, dim).reshape(shape)


def collect(shard, axis, dim):
    pieces = from_everyone(shard, axis)
    return in_order(pieces, dim)


def cut_along(shard, dim, devices):
    shape = shard.shape
    pieces = shard.reshape(*shape[:dim], devices, shape[dim] // devices, *shape[dim + 1 :])
    return jnp.moveaxis(pieces, dim, 0)


def sum_at_owner(shard, axis, dim):
    devices = lax.axis_size(axis)
    pieces = lax.all_to_all(cut_along(shard, dim, devices), axis, 0, 0, tiled=True)
    return jnp.sum(pieces, axis=0)


def total_of(shard, axes):
    lines = shard.reshape(-1, shard.shape[-1])
    padded = rows_for(lines, lax.axis_size(axes))
    whole = collect(sum_at_owner(padded, axes, 0), axes, 0)
    return lax.slice_in_dim(whole, 0, len(lines)).reshape(shard.shape)


def inner_rows(left, right_side):
    return lax.dot_general(
        left,
        right_side,
        (((0,), (0,)), ((), ())),
        precision=lax.Precision.HIGHEST,
        preferred_element_type=jnp.float32,
    )


def outer_cols(left, right_side):
    return lax.dot_general(
        left,
        right_side,
        (((1,), (1,)), ((), ())),
        precision=lax.Precision.HIGHEST,
        preferred_element_type=jnp.float32,
    )


def orthonormal_rows(proj, gram_sum):
    chol_low = jnp.linalg.cholesky(gram_sum)
    return lax.linalg.triangular_solve(
        chol_low, proj, left_side=False, lower=True, transpose_a=True
    )


def per_device(momentum, grad_acc, query_basis, hidden_t, out_grad):
    exchanged = lax.all_to_all(hidden_t, "fsdp", split_axis=0, concat_axis=1, tiled=True)
    micro_grad = jnp.dot(
        exchanged,
        lax.all_gather(out_grad, "fsdp", axis=0, tiled=True),
        preferred_element_type=jnp.float32,
    )
    buffer = momentum + grad_acc + micro_grad
    partial_proj = jnp.dot(
        buffer, query_basis, precision=lax.Precision.HIGHEST, preferred_element_type=jnp.float32
    )
    proj_whole = over_copies(partial_proj, "tp")
    gram_sum = total_of(inner_rows(proj_whole, proj_whole), "fsdp")
    orthonormal = orthonormal_rows(proj_whole, gram_sum)
    right_partial = inner_rows(buffer, orthonormal)
    right_factor = total_of(right_partial, "fsdp")
    squares = over_copies(jnp.sum(right_factor * right_factor, axis=0), "tp")
    column_scale = lax.rsqrt(squares / D + epsilon)
    query_next = right_factor * column_scale
    momentum_next = buffer - (1.0 - momentum_keep) * outer_cols(orthonormal, right_factor)
    update = math.sqrt(FF / RANK) * outer_cols(orthonormal, query_next)
    return (update, momentum_next, query_next)


def solution(mesh):
    return jax.shard_map(
        per_device,
        mesh=mesh,
        in_specs=(
            P("fsdp", "tp"),
            P("fsdp", "tp"),
            P("tp", None),
            P(None, "fsdp"),
            P("fsdp", "tp"),
        ),
        out_specs=(P("fsdp", "tp"), P("fsdp", "tp"), P("tp", None)),
        check_vma=False,
    )
```

profile of v0, /device:TPU:1, one launch (start us, length us, event | category | flops | bytes accessed | tf_op | source)
XLA Modules:
  0.0 658.9 jit_solution(2942576600352427315)
XLA Ops:
  7.9 128.4 %all_to_all.50 = bf16[64,224,128]{2,1,0:T(8,128)(2,1)} all-to-all(bf16[64,224,128]{2,1,0:T(8,128)(2,1)} %bitcast.81), channel_id=1, replica_groups=mesh['fsdp'=64,'tp'=4] {'fsdp'}, dimensions={0} | all-to-all | bytes 7340032 | tf_op jit(solution)/shard_map/all_to_all | solution.py:91
  136.4 97.9 %all-gather.2.cloned.1.call-done = bf16[8192,1024]{1,0:T(8,128)(2,1)} async-done(((bf16[128,1024]{1,0:T(8,128)(2,1)}), bf16[8192,1024]{1,0:T(8,128)(2,1)}) %all-gather.2.cloned.1.call-update) | async-done | bytes 16777232 | tf_op jit(solution)/shard_map/all_gather | solution.py:94
  234.3 11.0 %fusion.4 = f32[224,1024]{1,0:T(8,128)S(1)} fusion(bf16[8192,1024]{1,0:T(8,128)(2,1)} %all-gather.2.cloned.1.call-done, f32[224,1024]{1,0:T(8,128)S(1)} %copy-done.15, f32[224,1024]{1,0:T(8,128)} %param.6, bf16[64,224,128]{2,1,0:T(8,128)(2,1)} %all_to_all.50), kind=kOutput, calls=%fused_computation.9 | convolution fusion | flops 3758555136 | bytes 23199744 | tf_op jit(solution)/shard_map/dot_general | solution.py:92
  245.3 1.7 fusion.45
  247.2 29.3 %all_to_all.51 = f32[4,224,512]{2,1,0:T(8,128)} all-to-all(f32[4,224,512]{2,1,0:T(8,128)S(1)} %broadcast_in_dim.10), channel_id=1, replica_groups=mesh['fsdp'=64,'tp'=4] {'tp'}, dimensions={0} | all-to-all | bytes 3670016 | tf_op jit(solution)/shard_map/all_to_all | solution.py:19
  276.5 1.7 reduce_sum.45
  279.5 40.4 %all_to_all.52 = f32[64,8,512]{2,1,0:T(8,128)} all-to-all(f32[64,8,512]{2,1,0:T(8,128)S(1)} %fusion.8), channel_id=1, replica_groups=mesh['fsdp'=64,'tp'=4] {'fsdp'}, dimensions={0} | all-to-all | bytes 2097152 | tf_op jit(solution)/shard_map/all_to_all | solution.py:52
  322.3 6.6 %all-to-all-start.3 = ((f32[64,8,512]{2,1,0:T(8,128)}), f32[64,8,512]{2,1,0:T(8,128)S(1)}, u32[]{:S(2)}, u32[]{:S(2)}) async-start(f32[64,8,512]{2,1,0:T(8,128)} %broadcast_in_dim.11), calls=%async_computation.3 | async-start | bytes 2097152 | tf_op jit(solution)/shard_map/all_to_all | solution.py:19
  328.9 29.5 %all-to-all-done.3 = f32[64,8,512]{2,1,0:T(8,128)S(1)} async-done(((f32[64,8,512]{2,1,0:T(8,128)}), f32[64,8,512]{2,1,0:T(8,128)S(1)}, u32[]{:S(2)}, u32[]{:S(2)}) %all-to-all-start.3) | async-done | bytes 1048608 | tf_op jit(solution)/shard_map/all_to_all | solution.py:19
  359.7 1.4 fusion.7
  362.2 11.7 %cholesky.104 = f32[128,128]{1,0:T(8,128)S(1)} custom-call(f32[128,128]{1,0:T(8,128)S(1)} %cholesky.266), custom_call_target="Cholesky" | custom-call | tf_op jit(solution)/shard_map/jit(cholesky)/cholesky | solution.py:84
  374.1 9.8 %custom-call.30 = f32[1,128,128]{1,2,0:T(8,128)S(1)} custom-call(f32[1,128,128]{2,1,0:T(8,128)S(1)} %get-tuple-element.30), custom_call_target="InvertDiagBlocksLowerTriangular" | custom-call | tf_op jit(solution)/shard_map/jit(cholesky)/cholesky | solution.py:84
  386.4 11.7 %cholesky.217 = f32[128,128]{1,0:T(8,128)S(1)} custom-call(f32[128,128]{1,0:T(8,128)S(1)} %cholesky.270), custom_call_target="Cholesky" | custom-call | tf_op jit(solution)/shard_map/jit(cholesky)/cholesky | solution.py:84
  398.1 10.0 %custom-call.31 = f32[1,128,128]{1,2,0:T(8,128)S(1)} custom-call(f32[1,128,128]{2,1,0:T(8,128)S(1)} %get-tuple-element.27), custom_call_target="InvertDiagBlocksLowerTriangular" | custom-call | tf_op jit(solution)/shard_map/jit(cholesky)/cholesky | solution.py:84
  410.7 11.7 %cholesky.238 = f32[128,128]{1,0:T(8,128)S(1)} custom-call(f32[128,128]{1,0:T(8,128)S(1)} %cholesky.275), custom_call_target="Cholesky" | custom-call | tf_op jit(solution)/shard_map/jit(cholesky)/cholesky | solution.py:84
  423.7 9.8 %custom-call.32 = f32[1,128,128]{1,2,0:T(8,128)S(1)} custom-call(f32[1,128,128]{2,1,0:T(8,128)S(1)} %get-tuple-element.24), custom_call_target="InvertDiagBlocksLowerTriangular" | custom-call | tf_op jit(solution)/shard_map/jit(cholesky)/cholesky | solution.py:84
  435.8 11.7 %cholesky.255 = f32[128,128]{1,0:T(8,128)S(1)} custom-call(f32[128,128]{1,0:T(8,128)S(1)} %convolution_subtract_fusion.5), custom_call_target="Cholesky" | custom-call | tf_op jit(solution)/shard_map/jit(cholesky)/cholesky | solution.py:84
  452.0 2.7 select_select_fusion
  454.7 14.1 %while.1 = (s32[]{:T(128)}, f32[512,512]{1,0:T(8,128)}, s32[4,2]{0,1:T(2,128)S(1)}, f32[4,128,128]{2,1,0:T(8,128)}, s32[]{:T(128)}) while((s32[]{:T(128)}, f32[512,512]{1,0:T(8,128)}, s32[4,2]{0,1:T(2,128)S(1)}, f32[4,128,128]{2,1,0:T(8,128)}, s32[]{:T(128)}) %tuple.31), condition=%wide.while_cond, body=%wide.while_body.sunk | while | flops 2 | bytes 132705 | solution.py:85
  455.4 2.9 bitcast_dynamic-update-slice_fusion.2
  459.0 2.9 bitcast_dynamic-update-slice_fusion.2
  462.5 2.9 bitcast_dynamic-update-slice_fusion.2
  466.0 2.8 bitcast_dynamic-update-slice_fusion.2
  468.8 40.7 %custom-call.33 = f32[4,128,128]{1,2,0:T(8,128)} custom-call(f32[4,128,128]{2,1,0:T(8,128)} %get-tuple-element.10), custom_call_target="InvertDiagBlocksLowerTriangular" | custom-call | tf_op jit(solution)/shard_map/triangular_solve | solution.py:85
  517.9 1.9 fusion.29
  519.8 50.9 %all_to_all.53 = f32[64,16,512]{2,1,0:T(8,128)} all-to-all(f32[64,16,512]{2,1,0:T(8,128)S(1)} %bitcast.79), channel_id=1, replica_groups=mesh['fsdp'=64,'tp'=4] {'fsdp'}, dimensions={0} | all-to-all | bytes 4194304 | tf_op jit(solution)/shard_map/all_to_all | solution.py:52
  570.8 1.7 reduce_sum.47
  572.7 60.9 %all_to_all.54 = f32[64,16,512]{2,1,0:T(8,128)S(1)} all-to-all(f32[64,16,512]{2,1,0:T(8,128)S(1)} %broadcast_in_dim.12), channel_id=1, replica_groups=mesh['fsdp'=64,'tp'=4] {'fsdp'}, dimensions={0} | all-to-all | bytes 4194304 | tf_op jit(solution)/shard_map/all_to_all | solution.py:19
  635.8 6.4 all-to-all-start.6
  642.3 4.7 fusion.3
  647.0 1.8 broadcast_multiply_fusion
  648.8 3.1 convolution_multiply_fusion.1
  (81 shorter events, 31.0 us)
Async XLA Ops:
  7.2 238.1 %copy-start = (f32[1024,512]{1,0:T(8,128)S(1)}, f32[1024,512]{1,0:T(8,128)}, u32[]{:S(2)}) copy-start(f32[1024,512]{1,0:T(8,128)} %param.7) | copy-start | bytes 6291460
  7.2 227.1 %all-gather.2.cloned.1.call-start = ((), (), s32[]{:S(2)}) async-start(), calls=%async_computation.7 | async-start | bytes 17039360 | tf_op jit(solution)/shard_map/all_gather | solution.py:94
  7.9 226.4 %copy-start.15 = (f32[224,1024]{1,0:T(8,128)S(1)}, f32[224,1024]{1,0:T(8,128)}, u32[]{:S(2)}) copy-start(f32[224,1024]{1,0:T(8,128)} %param.5) | copy-start | bytes 2752516
  245.2 2.0 copy-start.3
  278.2 41.6 %copy-start.5 = (f32[224,512]{1,0:T(8,128)}, f32[224,512]{1,0:T(8,128)S(1)}, u32[]{:S(2)}) copy-start(f32[224,512]{1,0:T(8,128)S(1)} %reduce_sum.45) | copy-start | bytes 1376260
  322.3 36.1 %all-to-all-start.3 = ((f32[64,8,512]{2,1,0:T(8,128)}), f32[64,8,512]{2,1,0:T(8,128)S(1)}, u32[]{:S(2)}, u32[]{:S(2)}) async-start(f32[64,8,512]{2,1,0:T(8,128)} %broadcast_in_dim.11), calls=%async_computation.3 | async-start | bytes 2097152 | tf_op jit(solution)/shard_map/all_to_all | solution.py:19
  361.2 1.0 copy-start.14
  408.4 1.0 copy-start.7
  410.7 98.9 %copy-start.6 = (f32[224,512]{1,0:T(8,128)S(1)}, f32[224,512]{1,0:T(8,128)}, u32[]{:S(2)}) copy-start(f32[224,512]{1,0:T(8,128)} %copy-done.5) | copy-start | bytes 1376260
  454.7 63.1 %copy-start.4 = (f32[224,1024]{1,0:T(8,128)S(1)}, f32[224,1024]{1,0:T(8,128)}, u32[]{:S(2)}) copy-start(f32[224,1024]{1,0:T(8,128)} %copy-done.3) | copy-start | bytes 2752516
  510.7 9.1 %copy-start.8 = (f32[224,128]{1,0:T(8,128)}, f32[224,128]{1,0:T(8,128)S(1)}, u32[]{:S(2)}) copy-start(f32[224,128]{1,0:T(8,128)S(1)} %fusion.27) | copy-start | bytes 344068
  512.9 6.9 %copy-start.10 = (f32[224,128]{1,0:T(8,128)}, f32[224,128]{1,0:T(8,128)S(1)}, u32[]{:S(2)}) copy-start(f32[224,128]{1,0:T(8,128)S(1)} %fusion.32) | copy-start | bytes 344068
  515.3 4.5 copy-start.12
  633.7 1.3 copy-start.1
  635.0 7.3 %copy-start.9 = (f32[224,128]{1,0:T(8,128)S(1)}, f32[224,128]{1,0:T(8,128)}, u32[]{:S(2)}) copy-start(f32[224,128]{1,0:T(8,128)} %copy-done.8) | copy-start | bytes 344068
  635.0 7.3 %copy-start.11 = (f32[224,128]{1,0:T(8,128)S(1)}, f32[224,128]{1,0:T(8,128)}, u32[]{:S(2)}) copy-start(f32[224,128]{1,0:T(8,128)} %copy-done.10) | copy-start | bytes 344068
  635.0 7.3 %copy-start.13 = (f32[224,128]{1,0:T(8,128)S(1)}, f32[224,128]{1,0:T(8,128)}, u32[]{:S(2)}) copy-start(f32[224,128]{1,0:T(8,128)} %copy-done.12) | copy-start | bytes 344068
  635.8 11.1 %all-to-all-start.6 = ((f32[4,1,512]{2,1,0:T(1,128)}), f32[4,1,512]{2,1,0:T(1,128)S(1)}, u32[]{:S(2)}, u32[]{:S(2)}) async-start(f32[4,1,512]{2,1,0:T(1,128)} %broadcast_in_dim.13), calls=%async_computation.6 | async-start | bytes 16384 | tf_op jit(solution)/shard_map/all_to_all | solution.py:19
  648.8 3.1 copy-start.2
Sparse Core Ops, SparseCore 0:
  11.3 222.9 all-gather.1
where the time goes:
time: 667 us; the launch traced here: 659 us
  blocking collectives  310 us (46%)
  other arithmetic  132 us (20%)
  waiting for transfers between devices  128 us (19%)
  matrix products  37.8 us (6%)
  local copies, waits for them, and re-layouts  21.3 us (3%)
  between operations  17.2 us (3%)
  starting transfers between devices  13.1 us (2%)
    all_to_all x1, blocking collectives, per_device(): lax.all_to_all(hidden_t, 'fsdp', split_axis=0, concat_axis=1, tiled=True)  128 us
    all_gather x1, waiting for transfers between devices, per_device(): lax.all_gather(out_grad, 'fsdp', axis=0, tiled=True)  97.9 us
    all_to_all x2, blocking collectives, sum_at_owner(): lax.all_to_all(cut_along(shard, dim, devices), axis, 0, 0, tiled=True)  91.3 us
    all_to_all x2, blocking collectives, from_everyone(): lax.all_to_all(jnp.broadcast_to(shard[None], (devices, *shard.shape)), ax...  90.2 us
    another operation x14, other arithmetic, orthonormal_rows(): chol_low = jnp.linalg.cholesky(gram_sum)  79.8 us
    another operation x3, other arithmetic, orthonormal_rows(): lax.linalg.triangular_solve(chol_low, proj, left_side=False, lower=True,...  43.5 us
    all_to_all x2, waiting for transfers between devices, from_everyone(): lax.all_to_all(jnp.broadcast_to(shard[None], (devices, *shard.shape)), ax...  29.5 us
    another operation x12, local copies, waits for them, and re-layouts  14.1 us
  transfers between devices with their start and end apart: 3, of which 2 were waited for; matrix products, arithmetic and copies ran while one was open for 1% of the time, Pallas kernels for 0%

commit v1 on v0

v1 whole, which is shorter than its diff:
```python
import math

import jax
import jax.numpy as jnp
from jax import lax
from jax.experimental import pallas as pl
from jax.experimental.pallas import tpu as pltpu
from jax.sharding import Mesh
from jax.sharding import PartitionSpec as P

D = 4096
FF = 14336
RANK = 512
TILE = 128
SUB = 8
CHUNKS = 2

momentum_keep = 0.95
epsilon = 1e-06

ROWS = ("x", "y", "zh")
COLS = ("zl", "core")


def dot(left, right, left_dim, right_dim):
    return lax.dot_general(
        left,
        right,
        (((left_dim,), (right_dim,)), ((), ())),
        precision=lax.Precision.HIGHEST,
        preferred_element_type=jnp.float32,
    )


def eliminate(tile):
    lane = lax.broadcasted_iota(jnp.int32, (SUB, TILE), 1)
    sub = lax.broadcasted_iota(jnp.int32, (SUB, TILE), 0)
    x = [tile[SUB * i : SUB * i + SUB, :] for i in range(TILE // SUB)]
    for p in range(TILE // SUB):
        first = SUB * p
        below = range(p, TILE // SUB)
        cols = [
            {i: jnp.broadcast_to(x[i][:, first + k : first + k + 1], (SUB, TILE)) for i in below}
            for k in range(SUB)
        ]
        inside = (lane >= first) & (lane < first + SUB)
        for i in below:
            eye = (lane == sub + first).astype(jnp.float32) if i == p else 0.0
            x[i] = jnp.where(inside, eye, x[i])
        root = jnp.ones((SUB, TILE), jnp.float32)
        for k in range(SUB):
            pivot = jnp.broadcast_to(cols[k][p][k : k + 1, :], (SUB, TILE))
            inverse = 1.0 / pivot
            root = jnp.where(sub == k, lax.rsqrt(pivot), root)
            mult = {i: cols[k][i] * inverse for i in below}
            mult[p] = jnp.where(sub > k, mult[p], 0.0)
            for m in range(k + 1, SUB):
                head = jnp.broadcast_to(cols[m][p][k : k + 1, :], (SUB, TILE))
                for i in below:
                    cols[m][i] = cols[m][i] - mult[i] * head
            row = jnp.broadcast_to(x[p][k : k + 1, :], (SUB, TILE))
            for i in below:
                x[i] = x[i] - mult[i] * row
        x[p] = jnp.where(lane <= sub + first, x[p] * root, 0.0)
    return jnp.concatenate(x, axis=0)


def inverse_factor_kernel(gram_ref, out_ref, work, small):
    work[...] = gram_ref[...]
    out_ref[...] = jnp.zeros_like(out_ref)

    def step(b, carry):
        corner = pl.multiple_of(b * TILE, TILE)
        small[...] = eliminate(work[pl.ds(corner, TILE), pl.ds(corner, TILE)])
        for s in range(RANK // TILE):

            @pl.when(b == s)
            def _():
                at = s * TILE
                end = at + TILE
                inv = small[...]
                out_ref[at:end, at:end] = inv
                if s > 0:
                    done = dot(inv, work[at:end, :at], 1, 0)
                    out_ref[at:end, :at] = done
                if end < RANK:
                    rest = dot(inv, work[at:end, end:], 1, 0)
                    work[end:, end:] -= dot(rest, rest, 0, 0)
                    work[end:, at:end] = -dot(rest, inv, 0, 0)
                    if s > 0:
                        work[end:, :at] -= dot(rest, done, 0, 0)

        return carry

    lax.fori_loop(0, RANK // TILE, step, 0)


def inverse_factor(gram):
    return pl.pallas_call(
        inverse_factor_kernel,
        out_shape=jax.ShapeDtypeStruct((RANK, RANK), jnp.float32),
        in_specs=[pl.BlockSpec(memory_space=pltpu.VMEM)],
        out_specs=pl.BlockSpec(memory_space=pltpu.VMEM),
        scratch_shapes=[
            pltpu.VMEM((RANK, RANK), jnp.float32),
            pltpu.VMEM((TILE, TILE), jnp.float32),
        ],
        cost_estimate=pl.CostEstimate(
            flops=30_000_000_000, bytes_accessed=8 * RANK * RANK, transcendentals=0
        ),
        name="inverse_factor",
    )(gram)


def swap(pieces, axes):
    return lax.all_to_all(pieces, axes, 0, 0, tiled=True)


def to_all(piece, axes):
    devices = lax.axis_size(axes)
    return swap(jnp.broadcast_to(piece[None], (devices, *piece.shape)), axes)


def ring(by, turned=False):
    other = -by if turned else by
    return [(2 * z + c, 2 * ((z + (other if c else by)) % 4) + c) for z in range(4) for c in range(2)]


def neighbours(value, by):
    return lax.ppermute(value, ("zh", "core"), ring(by, turned=True))


def flip(value, axis):
    return lax.ppermute(value, axis, [(0, 1), (1, 0)])


def part(stack, index, dim=0):
    return lax.dynamic_index_in_dim(stack, index, dim, keepdims=False)


def sum_at_owner(stack, axis):
    me = lax.axis_index(axis)
    total = part(stack, me)
    arrived = []
    for by in range(1, 4):
        pairs = [(i, (i + by) % 4) for i in range(4)]
        arrived.append(lax.ppermute(part(stack, (me + by) % 4), axis, pairs))
    return total + arrived[0] + arrived[1] + arrived[2]


def summed_micro_grad(mine, other, grads):
    even = lax.axis_index("core") == 0

    def product(hidden):
        return lax.dot_general(
            hidden,
            grads.reshape(16, -1, grads.shape[1]),
            (((0, 3), (0, 1)), ((), ())),
            preferred_element_type=jnp.float32,
        )

    here, there = product(mine), product(other)
    own = jnp.where(even, here[0], there[0])
    across = jnp.where(even, there[0], here[0])
    ahead, behind = here[1], there[1]
    half = own.shape[0] // 2
    ahead_far = neighbours(across[:half], 1)
    behind_far = neighbours(across[half:], -1)
    from_ahead = neighbours(ahead[half:], 1)
    from_behind = neighbours(behind[:half], -1)
    from_ahead_far = neighbours(ahead[:half] + ahead_far, 1)
    from_behind_far = neighbours(behind[half:] + behind_far, -1)
    return jnp.concatenate(
        [own[:half] + from_behind + from_ahead_far, own[half:] + from_ahead + from_behind_far]
    )


def per_device(momentum, grad_acc, query_basis, hidden_t, out_grad):
    rows, features = momentum.shape
    tokens = hidden_t.shape[1]
    z, core = lax.axis_index("zh"), lax.axis_index("core")
    blocks = hidden_t.reshape(16, 4, rows, tokens)
    wanted = jnp.stack([part(blocks, (z + 2 * core + k) % 4, 1) for k in range(2)], axis=1)
    mine = swap(wanted, ("x", "y"))
    other = flip(mine, "core")
    width = features // CHUNKS
    buffers, partial_proj = [], 0.0
    for k in range(CHUNKS):
        at = slice(k * width, (k + 1) * width)
        grads = lax.all_gather(out_grad[:, at], ("x", "y"), axis=0, tiled=True)
        micro_grad = summed_micro_grad(mine, other, grads)
        buffers.append(momentum[:, at] + grad_acc[:, at] + micro_grad)
        partial_proj = partial_proj + dot(buffers[-1], query_basis[at], 1, 0)
    buffer = jnp.concatenate(buffers, axis=1)

    chip_proj = partial_proj + flip(partial_proj, "core")
    proj = chip_proj + flip(chip_proj, "zl")
    first = lax.axis_index(COLS) * TILE
    strip = dot(lax.dynamic_slice_in_dim(proj, first, TILE, 1), proj, 0, 0)
    tiles = strip.reshape(16, 8, 4, 128).transpose(0, 2, 1, 3).reshape(64, 8, 128)
    tiles = to_all(swap(tiles, ROWS).sum(axis=0), ROWS)
    strip = tiles.reshape(16, 4, 8, 128).transpose(0, 2, 1, 3).reshape(TILE, RANK)
    gram = to_all(strip, COLS).reshape(RANK, RANK)

    mixed = dot(buffer, proj, 0, 0)
    for axis in ROWS:
        mixed = sum_at_owner(mixed.reshape(4, -1, RANK), axis)
    mixed = to_all(mixed, "zh").reshape(-1, RANK)
    mixed = lax.all_gather(mixed, ("x", "y"), axis=0, tiled=True)

    inv = inverse_factor(gram)
    ortho = dot(proj, inv, 1, 1)
    right = dot(mixed, inv, 1, 1)
    squares = to_all(jnp.sum(right * right, axis=0)[None], COLS).sum(axis=(0, 1))
    momentum_next = buffer - (1.0 - momentum_keep) * dot(ortho, right, 1, 1)
    query_next = right * lax.rsqrt(squares / D + epsilon)
    update = math.sqrt(FF / RANK) * dot(ortho, query_next, 1, 1)
    return (update, momentum_next, query_next)


def solution(mesh):
    fine = Mesh(mesh.devices.reshape(4, 4, 4, 2, 2), ROWS + COLS)
    return jax.shard_map(
        per_device,
        mesh=fine,
        in_specs=(
            P(ROWS, COLS),
            P(ROWS, COLS),
            P(COLS, None),
            P(None, ROWS),
            P(ROWS, COLS),
        ),
        out_specs=(P(ROWS, COLS), P(ROWS, COLS), P(COLS, None)),
        check_vma=False,
    )
```

time: 667 us -> 382 us (0.57)
  blocking collectives: 310 us -> 20.6 us
  other arithmetic: 132 us -> 8.17 us
  starting transfers between devices: 13.1 us -> 95.3 us
  waiting for transfers between devices: 128 us -> 172 us
  Pallas kernels: 0 us -> 21.5 us
  matrix products: 37.8 us -> 29 us
  local copies, waits for them, and re-layouts: 21.3 us -> 13.8 us
    all_to_all x5 -> x1, blocking collectives: 310 us -> 20.6 us  [swap(): return lax.all_to_all(pieces, axes, 0, 0, tiled=True)]
    another operation x17 -> x1, other arithmetic: 123 us -> 1.4 us  [per_device(): jnp.stack([part(blocks, (z + 2 * core + k) % 4, 1) for k in range(2)], ax...]
    ppermute x0 -> x24, waiting for transfers between devices: none -> 56 us  [the longest x9 24.9 us: sum_at_owner(): arrived.append(lax.ppermute(part(stack, (me + by) % 4), axis, pairs))]
    ppermute x0 -> x24, starting transfers between devices: none -> 53.8 us  [the longest x12 32.3 us: neighbours(): return lax.ppermute(value, ('zh', 'core'), ring(by, turned=True))]
    all_gather x1 -> x3, waiting for transfers between devices: 97.9 us -> 67.1 us  [the longest x2 60 us: per_device(): grads = lax.all_gather(out_grad[:, at], ('x', 'y'), axis=0, tiled=True)]
    all_to_all x2 -> x5, starting transfers between devices: 13 us -> 41.4 us  [swap(): return lax.all_to_all(pieces, axes, 0, 0, tiled=True)]
    pallas_call x0 -> x1, Pallas kernels: none -> 21.5 us  [inverse_factor(): pl.pallas_call(inverse_factor_kernel, out_shape=jax.ShapeDtypeStruct((RAN...]
    all_to_all x2 -> x5, waiting for transfers between devices: 29.5 us -> 47.5 us  [swap(): return lax.all_to_all(pieces, axes, 0, 0, tiled=True)]
  transfers between devices with their start and end apart: 3 -> 32, of which waited for: 2 -> 18; matrix products, arithmetic and copies ran while one was open for 1% -> 7% of each run, Pallas kernels for 0% -> 6%
where the time goes in v1:
time: 382 us; the launch traced here: 375 us
  waiting for transfers between devices  172 us (45%)
  starting transfers between devices  95.3 us (25%)
  matrix products  29 us (8%)
  Pallas kernels  21.5 us (6%)
  blocking collectives  20.6 us (5%)
  between operations  14.4 us (4%)
  local copies, waits for them, and re-layouts  13.8 us (4%)
  other arithmetic  8.17 us (2%)
    all_gather x2, waiting for transfers between devices, per_device(): grads = lax.all_gather(out_grad[:, at], ('x', 'y'), axis=0, tiled=True)  60 us
    all_to_all x5, waiting for transfers between devices, swap(): return lax.all_to_all(pieces, axes, 0, 0, tiled=True)  47.5 us
    all_to_all x5, starting transfers between devices, swap(): return lax.all_to_all(pieces, axes, 0, 0, tiled=True)  41.4 us
    ppermute x12, starting transfers between devices, neighbours(): return lax.ppermute(value, ('zh', 'core'), ring(by, turned=True))  32.3 us
    ppermute x9, waiting for transfers between devices, sum_at_owner(): arrived.append(lax.ppermute(part(stack, (me + by) % 4), axis, pairs))  24.9 us
    pallas_call x1, Pallas kernels, inverse_factor(): pl.pallas_call(inverse_factor_kernel, out_shape=jax.ShapeDtypeStruct((RAN...  21.5 us
    all_to_all x1, blocking collectives, swap(): return lax.all_to_all(pieces, axes, 0, 0, tiled=True)  20.6 us
    ppermute x12, waiting for transfers between devices, neighbours(): return lax.ppermute(value, ('zh', 'core'), ring(by, turned=True))  18.8 us
  transfers between devices with their start and end apart: 32, of which 18 were waited for; matrix products, arithmetic and copies ran while one was open for 7% of the time, Pallas kernels for 6%

profile of v1, /device:TPU:1, one launch (start us, length us, event | category | flops | bytes accessed | tf_op | source)
XLA Modules:
  0.0 375.0 jit_solution(2074679594020975702)
XLA Ops:
  11.9 7.6 %all-to-all-start = ((bf16[16,2,224,128]{3,2,1,0:T(8,128)(2,1)}), bf16[16,2,224,128]{3,2,1,0:T(8,128)(2,1)S(1)}, u32[]{:S(2)}, u32[]{:S(2)}) async-start(bf16[16,2,224,128]{3,2,1,0:T(8,128)(2,1)} %pad_maximum_fusion), calls=%async_computation | async-start | bytes 3670016 | tf_op jit(solution)/shard_map/all_to_all | solution.py:116
  20.3 25.6 %all-to-all-done = bf16[16,2,224,128]{3,2,1,0:T(8,128)(2,1)S(1)} async-done(((bf16[16,2,224,128]{3,2,1,0:T(8,128)(2,1)}), bf16[16,2,224,128]{3,2,1,0:T(8,128)(2,1)S(1)}, u32[]{:S(2)}, u32[]{:S(2)}) %all-to-all-start) | async-done | bytes 1835040 | tf_op jit(solution)/shard_map/all_to_all | solution.py:116
  47.2 3.7 collective-permute-start
  50.9 23.9 %all-gather.6.cloned.1.call-done = bf16[2048,512]{1,0:T(8,128)(2,1)} async-done(((bf16[128,512]{1,0:T(8,128)(2,1)}), bf16[2048,512]{1,0:T(8,128)(2,1)}) %all-gather.6.cloned.1.call-update) | async-done | bytes 2097168 | tf_op jit(solution)/shard_map/all_gather | solution.py:190
  74.8 2.8 convolution_bitcast_fusion.1
  77.6 2.9 convolution_bitcast_fusion
  90.3 36.2 %all-gather.4.cloned.1.call-done = bf16[2048,512]{1,0:T(8,128)(2,1)} async-done(((bf16[128,512]{1,0:T(8,128)(2,1)}), bf16[2048,512]{1,0:T(8,128)(2,1)}) %all-gather.4.cloned.1.call-update) | async-done | bytes 2097168 | tf_op jit(solution)/shard_map/all_gather | solution.py:190
  126.5 3.4 convolution_bitcast_fusion.2
  139.5 11.2 %collective-permute-start.12 = (f32[112,512]{1,0:T(8,128)S(1)}, f32[112,512]{1,0:T(8,128)S(1)}, u32[]{:S(2)}, u32[]{:S(2)}) collective-permute-start(f32[112,512]{1,0:T(8,128)S(1)} %fusion.7), channel_id=1, source_target_pairs={{0,12},{1,5},{4,0},{5,9},{8,4},{9,13},{12,8},{13,1},{2,14},{3,7},{... | collective-permute-start | bytes 688136 | tf_op jit(solution)/shard_map/ppermute | solution.py:130
  150.9 4.5 %collective-permute-start.4 = (f32[112,512]{1,0:T(8,128)S(1)}, f32[112,512]{1,0:T(8,128)S(1)}, u32[]{:S(2)}, u32[]{:S(2)}) collective-permute-start(f32[112,512]{1,0:T(8,128)S(1)} %slice_bitcast_fusion.10), channel_id=1, source_target_pairs={{0,4},{1,13},{4,8},{5,1},{8,12},{9,5},{12,0},{13,9},{2,6},{3,15},{... | collective-permute-start | bytes 688136 | tf_op jit(solution)/shard_map/ppermute | solution.py:130
  156.6 2.7 collective-permute-start.3
  159.4 2.7 collective-permute-done.9
  162.2 9.2 %collective-permute-done.4 = f32[112,512]{1,0:T(8,128)S(1)} collective-permute-done((f32[112,512]{1,0:T(8,128)S(1)}, f32[112,512]{1,0:T(8,128)S(1)}, u32[]{:S(2)}, u32[]{:S(2)}) %collective-permute-start.4) | collective-permute-done | bytes 229408 | tf_op jit(solution)/shard_map/ppermute | solution.py:130
  171.4 6.0 %collective-permute-done.3 = f32[112,512]{1,0:T(8,128)S(1)} collective-permute-done((f32[112,512]{1,0:T(8,128)S(1)}, f32[112,512]{1,0:T(8,128)S(1)}, u32[]{:S(2)}, u32[]{:S(2)}) %collective-permute-start.3) | collective-permute-done | bytes 229408 | tf_op jit(solution)/shard_map/ppermute | solution.py:130
  183.0 2.5 collective-permute-start.14
  185.5 10.5 %collective-permute-done.14 = f32[224,512]{1,0:T(8,128)S(1)} collective-permute-done((f32[224,512]{1,0:T(8,128)S(1)}, f32[224,512]{1,0:T(8,128)S(1)}, u32[]{:S(2)}, u32[]{:S(2)}) %collective-permute-start.14) | collective-permute-done | bytes 458784 | tf_op jit(solution)/shard_map/ppermute | solution.py:134
  202.6 10.8 %collective-permute-done.15 = f32[256,512]{1,0:T(8,128)} collective-permute-done((f32[256,512]{1,0:T(8,128)}, f32[256,512]{1,0:T(8,128)}, u32[]{:S(2)}, u32[]{:S(2)}) %collective-permute-start.15) | collective-permute-done | bytes 524320 | tf_op jit(solution)/shard_map/ppermute | solution.py:147
  213.3 11.9 %collective-permute-done.16 = f32[256,512]{1,0:T(8,128)} collective-permute-done((f32[256,512]{1,0:T(8,128)}, f32[256,512]{1,0:T(8,128)}, u32[]{:S(2)}, u32[]{:S(2)}) %collective-permute-start.16) | collective-permute-done | bytes 524320 | tf_op jit(solution)/shard_map/ppermute | solution.py:147
  233.5 14.8 %all-to-all-start.1 = ((f32[64,8,128]{2,1,0:T(8,128)}), f32[64,8,128]{2,1,0:T(8,128)S(1)}, u32[]{:S(2)}, u32[]{:S(2)}) async-start(f32[64,8,128]{2,1,0:T(8,128)} %bitcast.33), calls=%async_computation.1 | async-start | bytes 524288 | tf_op jit(solution)/shard_map/all_to_all | solution.py:116
  251.7 2.8 collective-permute-start.22
  254.5 3.3 collective-permute-start.23
  262.1 3.3 all-to-all-start.4
  265.5 7.5 %all-to-all-done.4 = f32[4,16,512]{2,1,0:T(8,128)S(1)} async-done(((f32[4,16,512]{2,1,0:T(8,128)}), f32[4,16,512]{2,1,0:T(8,128)S(1)}, u32[]{:S(2)}, u32[]{:S(2)}) %all-to-all-start.4) | async-done | bytes 131104 | tf_op jit(solution)/shard_map/all_to_all | solution.py:116
  272.9 20.6 %all_to_all.30 = f32[64,8,128]{2,1,0:T(8,128)S(1)} all-to-all(f32[64,8,128]{2,1,0:T(8,128)S(1)} %broadcast_in_dim.10), channel_id=1, replica_groups=mesh['x'=4,'y'=4,'zh'=4,'zl'=2,'core'=2] {'x','y','zh'}, dimensions={0} | all-to-all | bytes 524288 | tf_op jit(solution)/shard_map/all_to_all | solution.py:116
  294.6 10.1 %all-to-all-start.3 = ((f32[4,128,512]{2,1,0:T(8,128)}), f32[4,128,512]{2,1,0:T(8,128)S(1)}, u32[]{:S(2)}, u32[]{:S(2)}) async-start(f32[4,128,512]{2,1,0:T(8,128)} %broadcast_in_dim.12), calls=%async_computation.3 | async-start | bytes 2097152 | tf_op jit(solution)/shard_map/all_to_all | solution.py:116
  305.4 12.9 %all-to-all-done.3 = f32[4,128,512]{2,1,0:T(8,128)S(1)} async-done(((f32[4,128,512]{2,1,0:T(8,128)}), f32[4,128,512]{2,1,0:T(8,128)S(1)}, u32[]{:S(2)}, u32[]{:S(2)}) %all-to-all-start.3) | async-done | bytes 1048608 | tf_op jit(solution)/shard_map/all_to_all | solution.py:116
  319.2 21.5 %inverse_factor.1 = f32[512,512]{1,0:T(8,128)} custom-call(f32[512,512]{1,0:T(8,128)} %bitcast.151), custom_call_target="tpu_custom_call" | custom-call | flops 30000001024 | bytes 2097152 | tf_op jit(solution)/shard_map/inverse_factor/pallas_call | solution.py:99
  343.1 7.1 %all-gather.8.cloned.1.call-done = f32[1024,512]{1,0:T(8,128)} async-done(((f32[64,512]{1,0:T(8,128)}), f32[1024,512]{1,0:T(8,128)}) %all-gather.8.cloned.1.call-update) | async-done | bytes 2097168 | tf_op jit(solution)/shard_map/all_gather | solution.py:209
  350.2 5.3 %multiply_reduce_fusion = (f32[512]{0:T(512)S(1)}, f32[1024,512]{1,0:T(8,128)S(1)}) fusion(f32[1024,512]{1,0:T(8,128)} %all-gather.8.cloned.1.call-done, f32[512,512]{1,0:T(8,128)} %inverse_factor.1), kind=kOutput, calls=%fused_computation | convolution fusion | flops 3222273536 | bytes 5244928 | tf_op jit(solution)/shard_map/dot_general | solution.py:26
  356.1 5.7 %all-to-all-start.5 = ((f32[4,1,512]{2,1,0:T(1,128)}), f32[4,1,512]{2,1,0:T(1,128)S(1)}, u32[]{:S(2)}, u32[]{:S(2)}) async-start(f32[4,1,512]{2,1,0:T(1,128)} %broadcast_in_dim.14), calls=%async_computation.5 | async-start | bytes 16384 | tf_op jit(solution)/shard_map/all_to_all | solution.py:116
  361.8 3.0 fusion
  365.2 3.1 convolution_multiply_fusion.1
  (104 shorter events, 61.7 us)
Async XLA Ops:
  7.2 67.6 %all-gather.6.cloned.1.call-start = ((), (), s32[]{:S(2)}) async-start(), calls=%async_computation.7 | async-start | bytes 2228224 | tf_op jit(solution)/shard_map/all_gather | solution.py:190
  11.9 33.9 %all-to-all-start = ((bf16[16,2,224,128]{3,2,1,0:T(8,128)(2,1)}), bf16[16,2,224,128]{3,2,1,0:T(8,128)(2,1)S(1)}, u32[]{:S(2)}, u32[]{:S(2)}) async-start(bf16[16,2,224,128]{3,2,1,0:T(8,128)(2,1)} %pad_maximum_fusion), calls=%async_computation | async-start | bytes 3670016 | tf_op jit(solution)/shard_map/all_to_all | solution.py:116
  19.5 107.0 %all-gather.4.cloned.1.call-start = ((), (), s32[]{:S(2)}) async-start(), calls=%async_computation.6 | async-start | bytes 2228224 | tf_op jit(solution)/shard_map/all_gather | solution.py:190
  47.2 30.4 %collective-permute-start = (bf16[16,2,224,128]{3,2,0,1:T(8,128)(2,1)}, bf16[16,2,224,128]{3,2,0,1:T(8,128)(2,1)}, u32[]{:S(2)}, u32[]{:S(2)}) collective-permute-start(bf16[16,2,224,128]{3,2,0,1:T(8,128)(2,1)} %copy.14), channel_id=1, source_target_pairs={{0,1},{1,0},{2,3},{3,2},{4,5},{5,4},{6,7},{7,6},{8,9},{9,8},{10,11... | collective-permute-start | bytes 5505032 | tf_op jit(solution)/shard_map/ppermute | solution.py:134
  81.5 52.1 %collective-permute-start.11 = (f32[112,512]{1,0:T(8,128)}, f32[112,512]{1,0:T(8,128)}, u32[]{:S(2)}, u32[]{:S(2)}) collective-permute-start(f32[112,512]{1,0:T(8,128)} %get-tuple-element.24), channel_id=1, source_target_pairs={{0,12},{1,5},{4,0},{5,9},{8,4},{9,13},{12,8},{13,1},{2,14},{3,7},{... | collective-permute-start | bytes 688136 | tf_op jit(solution)/shard_map/ppermute | solution.py:130
  83.8 52.6 %collective-permute-start.8 = (f32[112,512]{1,0:T(8,128)S(1)}, f32[112,512]{1,0:T(8,128)}, u32[]{:S(2)}, u32[]{:S(2)}) collective-permute-start(f32[112,512]{1,0:T(8,128)S(1)} %get-tuple-element.23), channel_id=1, source_target_pairs={{0,4},{1,13},{4,8},{5,1},{8,12},{9,5},{12,0},{13,9},{2,6},{3,15},{... | collective-permute-start | bytes 688136 | tf_op jit(solution)/shard_map/ppermute | solution.py:130
  86.1 64.9 %collective-permute-start.7 = (f32[112,512]{1,0:T(8,128)}, f32[112,512]{1,0:T(8,128)S(1)}, u32[]{:S(2)}, u32[]{:S(2)}) collective-permute-start(f32[112,512]{1,0:T(8,128)} %slice_bitcast_fusion.6), channel_id=1, source_target_pairs={{0,12},{1,5},{4,0},{5,9},{8,4},{9,13},{12,8},{13,1},{2,14},{3,7},{... | collective-permute-start | bytes 688136 | tf_op jit(solution)/shard_map/ppermute | solution.py:130
  88.7 66.8 %collective-permute-start.10 = (f32[112,512]{1,0:T(8,128)}, f32[112,512]{1,0:T(8,128)S(1)}, u32[]{:S(2)}, u32[]{:S(2)}) collective-permute-start(f32[112,512]{1,0:T(8,128)} %slice_bitcast_fusion.2), channel_id=1, source_target_pairs={{0,4},{1,13},{4,8},{5,1},{8,12},{9,5},{12,0},{13,9},{2,6},{3,15},{... | collective-permute-start | bytes 688136 | tf_op jit(solution)/shard_map/ppermute | solution.py:130
  131.2 8.3 %collective-permute-start.5 = (f32[112,512]{1,0:T(8,128)S(1)}, f32[112,512]{1,0:T(8,128)S(1)}, u32[]{:S(2)}, u32[]{:S(2)}) collective-permute-start(f32[112,512]{1,0:T(8,128)S(1)} %get-tuple-element.20), channel_id=1, source_target_pairs={{0,12},{1,5},{4,0},{5,9},{8,4},{9,13},{12,8},{13,1},{2,14},{3,7},{... | collective-permute-start | bytes 688136 | tf_op jit(solution)/shard_map/ppermute | solution.py:130
  133.6 17.2 %collective-permute-start.2 = (f32[112,512]{1,0:T(8,128)S(1)}, f32[112,512]{1,0:T(8,128)S(1)}, u32[]{:S(2)}, u32[]{:S(2)}) collective-permute-start(f32[112,512]{1,0:T(8,128)S(1)} %get-tuple-element.19), channel_id=1, source_target_pairs={{0,4},{1,13},{4,8},{5,1},{8,12},{9,5},{12,0},{13,9},{2,6},{3,15},{... | collective-permute-start | bytes 688136 | tf_op jit(solution)/shard_map/ppermute | solution.py:130
  136.3 25.9 %collective-permute-start.1 = (f32[112,512]{1,0:T(8,128)S(1)}, f32[112,512]{1,0:T(8,128)S(1)}, u32[]{:S(2)}, u32[]{:S(2)}) collective-permute-start(f32[112,512]{1,0:T(8,128)S(1)} %slice_bitcast_fusion.14), channel_id=1, source_target_pairs={{0,12},{1,5},{4,0},{5,9},{8,4},{9,13},{12,8},{13,1},{2,14},{3,7},{... | collective-permute-start | bytes 688136 | tf_op jit(solution)/shard_map/ppermute | solution.py:130
  139.5 17.1 %collective-permute-start.12 = (f32[112,512]{1,0:T(8,128)S(1)}, f32[112,512]{1,0:T(8,128)S(1)}, u32[]{:S(2)}, u32[]{:S(2)}) collective-permute-start(f32[112,512]{1,0:T(8,128)S(1)} %fusion.7), channel_id=1, source_target_pairs={{0,12},{1,5},{4,0},{5,9},{8,4},{9,13},{12,8},{13,1},{2,14},{3,7},{... | collective-permute-start | bytes 688136 | tf_op jit(solution)/shard_map/ppermute | solution.py:130
  150.8 11.3 %collective-permute-start.9 = (f32[112,512]{1,0:T(8,128)S(1)}, f32[112,512]{1,0:T(8,128)S(1)}, u32[]{:S(2)}, u32[]{:S(2)}) collective-permute-start(f32[112,512]{1,0:T(8,128)S(1)} %fusion.10), channel_id=1, source_target_pairs={{0,4},{1,13},{4,8},{5,1},{8,12},{9,5},{12,0},{13,9},{2,6},{3,15},{... | collective-permute-start | bytes 688136 | tf_op jit(solution)/shard_map/ppermute | solution.py:130
  150.9 20.5 %collective-permute-start.4 = (f32[112,512]{1,0:T(8,128)S(1)}, f32[112,512]{1,0:T(8,128)S(1)}, u32[]{:S(2)}, u32[]{:S(2)}) collective-permute-start(f32[112,512]{1,0:T(8,128)S(1)} %slice_bitcast_fusion.10), channel_id=1, source_target_pairs={{0,4},{1,13},{4,8},{5,1},{8,12},{9,5},{12,0},{13,9},{2,6},{3,15},{... | collective-permute-start | bytes 688136 | tf_op jit(solution)/shard_map/ppermute | solution.py:130
  155.4 15.9 %collective-permute-start.6 = (f32[112,512]{1,0:T(8,128)S(1)}, f32[112,512]{1,0:T(8,128)S(1)}, u32[]{:S(2)}, u32[]{:S(2)}) collective-permute-start(f32[112,512]{1,0:T(8,128)S(1)} %fusion.13), channel_id=1, source_target_pairs={{0,12},{1,5},{4,0},{5,9},{8,4},{9,13},{12,8},{13,1},{2,14},{3,7},{... | collective-permute-start | bytes 688136 | tf_op jit(solution)/shard_map/ppermute | solution.py:130
  156.6 20.8 %collective-permute-start.3 = (f32[112,512]{1,0:T(8,128)S(1)}, f32[112,512]{1,0:T(8,128)S(1)}, u32[]{:S(2)}, u32[]{:S(2)}) collective-permute-start(f32[112,512]{1,0:T(8,128)S(1)} %fusion.16), channel_id=1, source_target_pairs={{0,4},{1,13},{4,8},{5,1},{8,12},{9,5},{12,0},{13,9},{2,6},{3,15},{... | collective-permute-start | bytes 688136 | tf_op jit(solution)/shard_map/ppermute | solution.py:130
  181.1 1.9 collective-permute-start.13
  183.0 13.0 %collective-permute-start.14 = (f32[224,512]{1,0:T(8,128)S(1)}, f32[224,512]{1,0:T(8,128)S(1)}, u32[]{:S(2)}, u32[]{:S(2)}) collective-permute-start(f32[224,512]{1,0:T(8,128)S(1)} %add.237), channel_id=1, source_target_pairs={{0,2},{2,0},{1,3},{3,1},{4,6},{6,4},{5,7},{7,5},{8,10},{10,8},{9,1... | collective-permute-start | bytes 1376264 | tf_op jit(solution)/shard_map/ppermute | solution.py:134
  199.3 14.1 %collective-permute-start.15 = (f32[256,512]{1,0:T(8,128)}, f32[256,512]{1,0:T(8,128)}, u32[]{:S(2)}, u32[]{:S(2)}) collective-permute-start(f32[256,512]{1,0:T(8,128)} %get-tuple-element.5), channel_id=1, source_target_pairs={{0,64},{64,128},{128,192},{192,0},{1,65},{65,129},{129,193},{193,1... | collective-permute-start | bytes 1572872 | tf_op jit(solution)/shard_map/ppermute | solution.py:147
  200.1 25.0 %collective-permute-start.16 = (f32[256,512]{1,0:T(8,128)}, f32[256,512]{1,0:T(8,128)}, u32[]{:S(2)}, u32[]{:S(2)}) collective-permute-start(f32[256,512]{1,0:T(8,128)} %get-tuple-element.7), channel_id=1, source_target_pairs={{0,128},{64,192},{128,0},{192,64},{1,129},{65,193},{129,1},{193,65... | collective-permute-start | bytes 1572872 | tf_op jit(solution)/shard_map/ppermute | solution.py:147
  202.6 22.9 %collective-permute-start.17 = (f32[256,512]{1,0:T(8,128)}, f32[256,512]{1,0:T(8,128)}, u32[]{:S(2)}, u32[]{:S(2)}) collective-permute-start(f32[256,512]{1,0:T(8,128)} %get-tuple-element.6), channel_id=1, source_target_pairs={{0,192},{64,0},{128,64},{192,128},{1,193},{65,1},{129,65},{193,129... | collective-permute-start | bytes 1572872 | tf_op jit(solution)/shard_map/ppermute | solution.py:147
  228.8 19.4 %collective-permute-start.18 = (f32[64,512]{1,0:T(8,128)S(1)}, f32[64,512]{1,0:T(8,128)S(1)}, u32[]{:S(2)}, u32[]{:S(2)}) collective-permute-start(f32[64,512]{1,0:T(8,128)S(1)} %get-tuple-element.14), channel_id=1, source_target_pairs={{0,16},{16,32},{32,48},{48,0},{1,17},{17,33},{33,49},{49,1},{2,18}... | collective-permute-start | bytes 393224 | tf_op jit(solution)/shard_map/ppermute | solution.py:147
  229.8 18.5 %collective-permute-start.19 = (f32[64,512]{1,0:T(8,128)S(1)}, f32[64,512]{1,0:T(8,128)S(1)}, u32[]{:S(2)}, u32[]{:S(2)}) collective-permute-start(f32[64,512]{1,0:T(8,128)S(1)} %get-tuple-element.16), channel_id=1, source_target_pairs={{0,32},{16,48},{32,0},{48,16},{1,33},{17,49},{33,1},{49,17},{2,34}... | collective-permute-start | bytes 393224 | tf_op jit(solution)/shard_map/ppermute | solution.py:147
  232.2 16.1 %collective-permute-start.20 = (f32[64,512]{1,0:T(8,128)S(1)}, f32[64,512]{1,0:T(8,128)S(1)}, u32[]{:S(2)}, u32[]{:S(2)}) collective-permute-start(f32[64,512]{1,0:T(8,128)S(1)} %get-tuple-element.15), channel_id=1, source_target_pairs={{0,48},{16,0},{32,16},{48,32},{1,49},{17,1},{33,17},{49,33},{2,50}... | collective-permute-start | bytes 393224 | tf_op jit(solution)/shard_map/ppermute | solution.py:147
  233.5 27.9 %all-to-all-start.1 = ((f32[64,8,128]{2,1,0:T(8,128)}), f32[64,8,128]{2,1,0:T(8,128)S(1)}, u32[]{:S(2)}, u32[]{:S(2)}) async-start(f32[64,8,128]{2,1,0:T(8,128)} %bitcast.33), calls=%async_computation.1 | async-start | bytes 524288 | tf_op jit(solution)/shard_map/all_to_all | solution.py:116
  249.3 8.5 %collective-permute-start.21 = (f32[16,512]{1,0:T(8,128)S(1)}, f32[16,512]{1,0:T(8,128)S(1)}, u32[]{:S(2)}, u32[]{:S(2)}) collective-permute-start(f32[16,512]{1,0:T(8,128)S(1)} %get-tuple-element.27), channel_id=1, source_target_pairs={{0,4},{4,8},{8,12},{12,0},{1,5},{5,9},{9,13},{13,1},{2,6},{6,10},{... | collective-permute-start | bytes 98312 | tf_op jit(solution)/shard_map/ppermute | solution.py:147
  251.7 8.1 %collective-permute-start.22 = (f32[16,512]{1,0:T(8,128)S(1)}, f32[16,512]{1,0:T(8,128)S(1)}, u32[]{:S(2)}, u32[]{:S(2)}) collective-permute-start(f32[16,512]{1,0:T(8,128)S(1)} %get-tuple-element.29), channel_id=1, source_target_pairs={{0,8},{4,12},{8,0},{12,4},{1,9},{5,13},{9,1},{13,5},{2,10},{6,14},... | collective-permute-start | bytes 98312 | tf_op jit(solution)/shard_map/ppermute | solution.py:147
  254.5 5.3 %collective-permute-start.23 = (f32[16,512]{1,0:T(8,128)S(1)}, f32[16,512]{1,0:T(8,128)S(1)}, u32[]{:S(2)}, u32[]{:S(2)}) collective-permute-start(f32[16,512]{1,0:T(8,128)S(1)} %get-tuple-element.28), channel_id=1, source_target_pairs={{0,12},{4,0},{8,4},{12,8},{1,13},{5,1},{9,5},{13,9},{2,14},{6,2},{... | collective-permute-start | bytes 98312 | tf_op jit(solution)/shard_map/ppermute | solution.py:147
  262.1 10.9 %all-to-all-start.4 = ((f32[4,16,512]{2,1,0:T(8,128)}), f32[4,16,512]{2,1,0:T(8,128)S(1)}, u32[]{:S(2)}, u32[]{:S(2)}) async-start(f32[4,16,512]{2,1,0:T(8,128)} %broadcast_in_dim.13), calls=%async_computation.4 | async-start | bytes 262144 | tf_op jit(solution)/shard_map/all_to_all | solution.py:116
  294.6 23.6 %all-to-all-start.3 = ((f32[4,128,512]{2,1,0:T(8,128)}), f32[4,128,512]{2,1,0:T(8,128)S(1)}, u32[]{:S(2)}, u32[]{:S(2)}) async-start(f32[4,128,512]{2,1,0:T(8,128)} %broadcast_in_dim.12), calls=%async_computation.3 | async-start | bytes 2097152 | tf_op jit(solution)/shard_map/all_to_all | solution.py:116
  304.7 45.5 %all-gather.8.cloned.1.call-start = ((), (), s32[]{:S(2)}) async-start(), calls=%async_computation.8 | async-start | bytes 2228224 | tf_op jit(solution)/shard_map/all_gather | solution.py:209
  356.1 8.8 %all-to-all-start.5 = ((f32[4,1,512]{2,1,0:T(1,128)}), f32[4,1,512]{2,1,0:T(1,128)S(1)}, u32[]{:S(2)}, u32[]{:S(2)}) async-start(f32[4,1,512]{2,1,0:T(1,128)} %broadcast_in_dim.14), calls=%async_computation.5 | async-start | bytes 16384 | tf_op jit(solution)/shard_map/all_to_all | solution.py:116
  (10 other events, 105.7 us)
Sparse Core Ops, SparseCore 0:
  11.0 63.7 all-gather.5
  77.2 49.3 all-gather.3
  308.5 41.6 all-gather.7
